TPU v7x, 32 devices: a whole 2x2x4 slice. The times are simulated.
32 devices in a mesh: freq: 8 (over y, x, core), feed: 4 (over z).
Axes of the slice: x: 2, y: 2, z: 4, core: 2. Of those that a mesh axis runs over, the one named last changes fastest.
Arguments:
- voltages: int32 [32, 2048, 2, 768], P(None, ('feed', 'freq')), may hold values from -127 to 127
- gains: float32 [2, 32, 2048], P(None, None, ('feed', 'freq')), may hold values from -0.06 to 0.06
Outputs:
- visibilities: float32 [32, 2, 2048, 2048], P('freq', None, 'feed')
All inputs are finite; a program needn't handle non-finite values.
Results may differ from a plain program's by a relative error of at most 0.0031.
Values may be sent and summed in bfloat16 or wider, within the bound.
A program may use at most 192 MiB of HBM per device.

v0:
```python
import jax
import jax.numpy as jnp
from jax import lax
from jax.sharding import PartitionSpec as P

def stack_rows(own_rows, samples):
    real_part = own_rows[..., :samples]
    imag_part = own_rows[..., samples:]
    swapped = jnp.concatenate([imag_part, -real_part], axis=-1)
    return jnp.stack([own_rows, swapped], axis=0)


def correlate(stacked, columns, samples):
    product = jnp.einsum("qrk,fk->qrf", stacked, columns, preferred_element_type=jnp.float32)
    return product * (1.0 / samples)


def ring_blocks(own, count):
    forward = [(source, (source + 1) % count) for source in range(count)]
    backward = [(source, (source - 1) % count) for source in range(count)]
    half = own.shape[0] // 2
    pieces = [(0, 0, own)]
    from_left = from_right = own
    for step in range(1, count):
        if 2 * step > count:
            break
        if 2 * step == count:
            pieces.append((-step, 0, lax.ppermute(from_left[:half], "feed", forward)))
            pieces.append((-step, half, lax.ppermute(from_right[half:], "feed", backward)))
        else:
            from_left = lax.ppermute(from_left, "feed", forward)
            from_right = lax.ppermute(from_right, "feed", backward)
            pieces.append((-step, 0, from_left))
            pieces.append((step, 0, from_right))
    return pieces


def per_device(voltages, gains):
    channels, local_feeds, _, samples = voltages.shape
    freq_count = lax.axis_size("freq")
    feed_count = lax.axis_size("feed")
    position = lax.axis_index("feed")
    owned = channels // freq_count
    rows = local_feeds * freq_count
    volts = voltages.reshape(freq_count, owned, local_feeds, 2, samples)
    scale = gains.reshape(2, freq_count, owned, local_feeds)[..., None]
    visibilities = jnp.zeros((owned, 2, rows, rows * feed_count), jnp.float32)
    for channel in range(owned):
        volt_real = volts[:, channel, :, 0].astype(jnp.float32)
        volt_imag = volts[:, channel, :, 1].astype(jnp.float32)
        gain_real = scale[0, :, channel]
        gain_imag = scale[1, :, channel]
        eq_real = gain_real * volt_real - gain_imag * volt_imag
        eq_imag = gain_real * volt_imag + gain_imag * volt_real
        blocks = jnp.concatenate([eq_real, eq_imag], axis=-1).astype(jnp.bfloat16)
        arrived = lax.all_to_all(blocks, "freq", split_axis=0, concat_axis=0, tiled=True)
        own_rows = arrived.reshape(rows, 2 * samples)
        stacked = stack_rows(own_rows, samples)
        for offset, start, block in ring_blocks(own_rows, feed_count):
            owner = lax.rem(position + offset + feed_count, feed_count)
            visibilities = lax.dynamic_update_slice(
                visibilities,
                correlate(stacked, block, samples)[None],
                (channel, 0, 0, owner * rows + start),
            )
    return visibilities


def solution(mesh):
    in_specs = (P(None, ("feed", "freq"), None, None), P(None, None, ("feed", "freq")))
    out_specs = P("freq", None, "feed", None)
    return jax.shard_map(
        per_device, mesh=mesh, in_specs=in_specs, out_specs=out_specs, check_vma=False
    )
```

profile of v0, /device:TPU:0, one launch (start us, length us, event | category | flops | bytes accessed | tf_op | source)
XLA Modules:
  0.0 488.0 jit_solution(5399585686346752361)
XLA Ops:
  0.0 17.9 %fusion.40 = (s32[8,1,64,1,768]{4,3,2,1,0:T(1,128)S(1)}, s32[8,1,64,1,768]{4,3,2,1,0:T(1,128)S(1)}, s32[8,1,64,1,768]{4,3,2,1,0:T(1,128)}, s32[8,1,64,1,768]{4,3...) fusion(s32[8,4,64,2,768]{4,3,2,1,0:T(2,128)} %bitcast.190), kind=kLoop, calls=%fused_computation.92 | loop fusion | bytes 25165824 | tf_op jit(solution)/shard_map/slice | solution.py:50
  21.3 5.2 %all-to-all-start = ((bf16[8,64,1536]{2,1,0:T(8,128)(2,1)}), bf16[8,64,1536]{2,1,0:T(8,128)(2,1)}, u32[]{:S(2)}, u32[]{:S(2)}) async-start(bf16[8,64,1536]{2,1,0:T(8,128)(2,1)} %pad_maximum_fusion.4), calls=%async_computation | async-start | bytes 3145728 | tf_op jit(solution)/shard_map/all_to_all | solution.py:56
  29.2 18.4 %all-to-all-done = bf16[8,64,1536]{2,1,0:T(8,128)(2,1)} async-done(((bf16[8,64,1536]{2,1,0:T(8,128)(2,1)}), bf16[8,64,1536]{2,1,0:T(8,128)(2,1)}, u32[]{:S(2)}, u32[]{:S(2)}) %all-to-all-start) | async-done | bytes 1572896 | tf_op jit(solution)/shard_map/all_to_all | solution.py:56
  47.6 4.3 all-to-all-start.1
  51.9 3.9 subtract_convert_fusion
  57.1 15.8 %all-to-all-done.1 = bf16[8,64,1536]{2,1,0:T(8,128)(2,1)} async-done(((bf16[8,64,1536]{2,1,0:T(8,128)(2,1)}), bf16[8,64,1536]{2,1,0:T(8,128)(2,1)}, u32[]{:S(2)}, u32[]{:S(2)}) %all-to-all-start.1) | async-done | bytes 1572896 | tf_op jit(solution)/shard_map/all_to_all | solution.py:56
  72.9 3.6 all-to-all-start.2
  82.1 15.4 %all-to-all-done.2 = bf16[8,64,1536]{2,1,0:T(8,128)(2,1)S(1)} async-done(((bf16[8,64,1536]{2,1,0:T(8,128)(2,1)}), bf16[8,64,1536]{2,1,0:T(8,128)(2,1)S(1)}, u32[]{:S(2)}, u32[]{:S(2)}) %all-to-all-start.2) | async-done | bytes 1572896 | tf_op jit(solution)/shard_map/all_to_all | solution.py:56
  97.5 3.6 all-to-all-start.3
  101.1 4.1 collective-permute-start.5
  111.9 4.4 collective-permute-done
  116.3 35.7 %collective-permute-start.9 = (bf16[512,1536]{1,0:T(8,128)(2,1)S(1)}, bf16[512,1536]{1,0:T(8,128)(2,1)}, u32[]{:S(2)}, u32[]{:S(2)}) collective-permute-start(bf16[512,1536]{1,0:T(8,128)(2,1)S(1)} %bitcast.202), channel_id=1, source_target_pairs={{0,3},{1,0},{2,1},{3,2},{4,7},{5,4},{6,5},{7,6},{8,11},{9,8},{10,9... | collective-permute-start | bytes 4718600 | tf_op jit(solution)/shard_map/ppermute | solution.py:32
  152.0 31.8 %collective-permute-done.4 = bf16[512,1536]{1,0:T(8,128)(2,1)} collective-permute-done((bf16[512,1536]{1,0:T(8,128)(2,1)}, bf16[512,1536]{1,0:T(8,128)(2,1)}, u32[]{:S(2)}, u32[]{:S(2)}) %collective-permute-start.4) | collective-permute-done | bytes 1572896 | tf_op jit(solution)/shard_map/ppermute | solution.py:31
  183.8 35.6 %collective-permute-start.13 = (bf16[512,1536]{1,0:T(8,128)(2,1)S(1)}, bf16[512,1536]{1,0:T(8,128)(2,1)}, u32[]{:S(2)}, u32[]{:S(2)}) collective-permute-start(bf16[512,1536]{1,0:T(8,128)(2,1)S(1)} %bitcast.192), channel_id=1, source_target_pairs={{0,3},{1,0},{2,1},{3,2},{4,7},{5,4},{6,5},{7,6},{8,11},{9,8},{10,9... | collective-permute-start | bytes 4718600 | tf_op jit(solution)/shard_map/ppermute | solution.py:32
  221.6 4.1 broadcast_in_dim.63
  225.7 3.7 bitcast_dynamic-update-slice_fusion.11
  237.7 13.5 %collective-permute-done.8 = bf16[512,1536]{1,0:T(8,128)(2,1)} collective-permute-done((bf16[512,1536]{1,0:T(8,128)(2,1)S(1)}, bf16[512,1536]{1,0:T(8,128)(2,1)}, u32[]{:S(2)}, u32[]{:S(2)}) %collective-permute-start.8) | collective-permute-done | bytes 1572896 | tf_op jit(solution)/shard_map/ppermute | solution.py:31
  251.2 35.6 %collective-permute-start.3 = (bf16[256,1536]{1,0:T(8,128)(2,1)}, bf16[256,1536]{1,0:T(8,128)(2,1)}, u32[]{:S(2)}, u32[]{:S(2)}) collective-permute-start(bf16[256,1536]{1,0:T(8,128)(2,1)} %slice.135), channel_id=1, source_target_pairs={{0,3},{1,0},{2,1},{3,2},{4,7},{5,4},{6,5},{7,6},{8,11},{9,8},{10,9... | collective-permute-start | bytes 2359304 | tf_op jit(solution)/shard_map/ppermute | solution.py:29
  291.0 27.7 %collective-permute-done.12 = bf16[512,1536]{1,0:T(8,128)(2,1)} collective-permute-done((bf16[512,1536]{1,0:T(8,128)(2,1)S(1)}, bf16[512,1536]{1,0:T(8,128)(2,1)}, u32[]{:S(2)}, u32[]{:S(2)}) %collective-permute-start.12) | collective-permute-done | bytes 1572896 | tf_op jit(solution)/shard_map/ppermute | solution.py:31
  318.7 35.5 %collective-permute-start.7 = (bf16[256,1536]{1,0:T(8,128)(2,1)}, bf16[256,1536]{1,0:T(8,128)(2,1)}, u32[]{:S(2)}, u32[]{:S(2)}) collective-permute-start(bf16[256,1536]{1,0:T(8,128)(2,1)} %slice.143), channel_id=1, source_target_pairs={{0,3},{1,0},{2,1},{3,2},{4,7},{5,4},{6,5},{7,6},{8,11},{9,8},{10,9... | collective-permute-start | bytes 2359304 | tf_op jit(solution)/shard_map/ppermute | solution.py:29
  358.4 3.7 bitcast_dynamic-update-slice_fusion.10
  362.1 3.7 bitcast_dynamic-update-slice_fusion.9
  365.8 3.4 collective-permute-done.2
  369.3 18.6 %collective-permute-start.11 = (bf16[256,1536]{1,0:T(8,128)(2,1)}, bf16[256,1536]{1,0:T(8,128)(2,1)}, u32[]{:S(2)}, u32[]{:S(2)}) collective-permute-start(bf16[256,1536]{1,0:T(8,128)(2,1)} %slice.151), channel_id=1, source_target_pairs={{0,3},{1,0},{2,1},{3,2},{4,7},{5,4},{6,5},{7,6},{8,11},{9,8},{10,9... | collective-permute-start | bytes 2359304 | tf_op jit(solution)/shard_map/ppermute | solution.py:29
  393.2 3.7 bitcast_dynamic-update-slice_fusion.8
  396.9 3.7 bitcast_dynamic-update-slice_fusion.7
  400.7 3.8 bitcast_dynamic-update-slice_fusion.6
  404.5 17.1 %collective-permute-start.15 = (bf16[256,1536]{1,0:T(8,128)(2,1)S(1)}, bf16[256,1536]{1,0:T(8,128)(2,1)S(1)}, u32[]{:S(2)}, u32[]{:S(2)}) collective-permute-start(bf16[256,1536]{1,0:T(8,128)(2,1)S(1)} %copy-done.6), channel_id=1, source_target_pairs={{0,3},{1,0},{2,1},{3,2},{4,7},{5,4},{6,5},{7,6},{8,11},{9,8},{10,9... | collective-permute-start | bytes 2359304 | tf_op jit(solution)/shard_map/ppermute | solution.py:29
  428.7 3.2 bitcast_dynamic-update-slice_fusion.4
  438.9 14.3 %collective-permute-done.11 = bf16[256,1536]{1,0:T(8,128)(2,1)} collective-permute-done((bf16[256,1536]{1,0:T(8,128)(2,1)}, bf16[256,1536]{1,0:T(8,128)(2,1)}, u32[]{:S(2)}, u32[]{:S(2)}) %collective-permute-start.11) | collective-permute-done | bytes 786464 | tf_op jit(solution)/shard_map/ppermute | solution.py:29
  463.6 6.9 %collective-permute-done.14 = bf16[256,1536]{1,0:T(8,128)(2,1)} collective-permute-done((bf16[256,1536]{1,0:T(8,128)(2,1)}, bf16[256,1536]{1,0:T(8,128)(2,1)}, u32[]{:S(2)}, u32[]{:S(2)}) %collective-permute-start.14) | collective-permute-done | bytes 786464 | tf_op jit(solution)/shard_map/ppermute | solution.py:28
  472.7 13.3 %collective-permute-done.15 = bf16[256,1536]{1,0:T(8,128)(2,1)S(1)} collective-permute-done((bf16[256,1536]{1,0:T(8,128)(2,1)S(1)}, bf16[256,1536]{1,0:T(8,128)(2,1)S(1)}, u32[]{:S(2)}, u32[]{:S(2)}) %collective-permute-start.15) | collective-permute-done | bytes 786464 | tf_op jit(solution)/shard_map/ppermute | solution.py:29
  (69 shorter events, 72.3 us)
Async XLA Ops:
  0.0 17.9 %copy-start.7 = (f32[2,32,64]{2,1,0:T(8,128)S(1)}, f32[2,32,64]{2,1,0:T(8,128)}, u32[]{:S(2)}) copy-start(f32[2,32,64]{2,1,0:T(8,128)} %param.3) | copy-start | bytes 49156
  21.3 26.3 %all-to-all-start = ((bf16[8,64,1536]{2,1,0:T(8,128)(2,1)}), bf16[8,64,1536]{2,1,0:T(8,128)(2,1)}, u32[]{:S(2)}, u32[]{:S(2)}) async-start(bf16[8,64,1536]{2,1,0:T(8,128)(2,1)} %pad_maximum_fusion.4), calls=%async_computation | async-start | bytes 3145728 | tf_op jit(solution)/shard_map/all_to_all | solution.py:56
  47.6 25.3 %all-to-all-start.1 = ((bf16[8,64,1536]{2,1,0:T(8,128)(2,1)}), bf16[8,64,1536]{2,1,0:T(8,128)(2,1)}, u32[]{:S(2)}, u32[]{:S(2)}) async-start(bf16[8,64,1536]{2,1,0:T(8,128)(2,1)} %pad_maximum_fusion.5), calls=%async_computation.1 | async-start | bytes 3145728 | tf_op jit(solution)/shard_map/all_to_all | solution.py:56
  57.1 23.7 %copy-start.1 = (bf16[8,64,768]{2,1,0:T(8,128)(2,1)S(1)}, bf16[8,64,768]{2,1,0:T(8,128)(2,1)}, u32[]{:S(2)}) copy-start(bf16[8,64,768]{2,1,0:T(8,128)(2,1)} %get-tuple-element.13) | copy-start | bytes 2359300
  57.1 23.7 %copy-start.2 = (bf16[8,64,768]{2,1,0:T(8,128)(2,1)S(1)}, bf16[8,64,768]{2,1,0:T(8,128)(2,1)}, u32[]{:S(2)}) copy-start(bf16[8,64,768]{2,1,0:T(8,128)(2,1)} %get-tuple-element.14) | copy-start | bytes 2359300
  72.9 24.5 %all-to-all-start.2 = ((bf16[8,64,1536]{2,1,0:T(8,128)(2,1)}), bf16[8,64,1536]{2,1,0:T(8,128)(2,1)S(1)}, u32[]{:S(2)}, u32[]{:S(2)}) async-start(bf16[8,64,1536]{2,1,0:T(8,128)(2,1)} %pad_maximum_fusion.6), calls=%async_computation.2 | async-start | bytes 3145728 | tf_op jit(solution)/shard_map/all_to_all | solution.py:56
  76.5 39.8 %collective-permute-start = (bf16[512,1536]{1,0:T(8,128)(2,1)}, bf16[512,1536]{1,0:T(8,128)(2,1)}, u32[]{:S(2)}, u32[]{:S(2)}) collective-permute-start(bf16[512,1536]{1,0:T(8,128)(2,1)} %bitcast.7), channel_id=1, source_target_pairs={{0,1},{1,2},{2,3},{3,0},{4,5},{5,6},{6,7},{7,4},{8,9},{9,10},{10,1... | collective-permute-start | bytes 4718600 | tf_op jit(solution)/shard_map/ppermute | solution.py:31
  78.7 73.3 %collective-permute-start.1 = (bf16[512,1536]{1,0:T(8,128)(2,1)}, bf16[512,1536]{1,0:T(8,128)(2,1)}, u32[]{:S(2)}, u32[]{:S(2)}) collective-permute-start(bf16[512,1536]{1,0:T(8,128)(2,1)} %bitcast.7), channel_id=1, source_target_pairs={{0,3},{1,0},{2,1},{3,2},{4,7},{5,4},{6,5},{7,6},{8,11},{9,8},{10,9... | collective-permute-start | bytes 4718600 | tf_op jit(solution)/shard_map/ppermute | solution.py:32
  80.8 103.0 %collective-permute-start.4 = (bf16[512,1536]{1,0:T(8,128)(2,1)}, bf16[512,1536]{1,0:T(8,128)(2,1)}, u32[]{:S(2)}, u32[]{:S(2)}) collective-permute-start(bf16[512,1536]{1,0:T(8,128)(2,1)} %bitcast.24), channel_id=1, source_target_pairs={{0,1},{1,2},{2,3},{3,0},{4,5},{5,6},{6,7},{7,4},{8,9},{9,10},{10,1... | collective-permute-start | bytes 4718600 | tf_op jit(solution)/shard_map/ppermute | solution.py:31
  97.5 54.5 %all-to-all-start.3 = ((bf16[8,64,1536]{2,1,0:T(8,128)(2,1)}), bf16[8,64,1536]{2,1,0:T(8,128)(2,1)S(1)}, u32[]{:S(2)}, u32[]{:S(2)}) async-start(bf16[8,64,1536]{2,1,0:T(8,128)(2,1)} %pad_maximum_fusion.7), calls=%async_computation.3 | async-start | bytes 3145728 | tf_op jit(solution)/shard_map/all_to_all | solution.py:56
  101.1 134.5 %collective-permute-start.5 = (bf16[512,1536]{1,0:T(8,128)(2,1)}, bf16[512,1536]{1,0:T(8,128)(2,1)}, u32[]{:S(2)}, u32[]{:S(2)}) collective-permute-start(bf16[512,1536]{1,0:T(8,128)(2,1)} %bitcast.24), channel_id=1, source_target_pairs={{0,3},{1,0},{2,1},{3,2},{4,7},{5,4},{6,5},{7,6},{8,11},{9,8},{10,9... | collective-permute-start | bytes 4718600 | tf_op jit(solution)/shard_map/ppermute | solution.py:32
  105.2 146.0 %collective-permute-start.8 = (bf16[512,1536]{1,0:T(8,128)(2,1)S(1)}, bf16[512,1536]{1,0:T(8,128)(2,1)}, u32[]{:S(2)}, u32[]{:S(2)}) collective-permute-start(bf16[512,1536]{1,0:T(8,128)(2,1)S(1)} %bitcast.200), channel_id=1, source_target_pairs={{0,1},{1,2},{2,3},{3,0},{4,5},{5,6},{6,7},{7,4},{8,9},{9,10},{10,1... | collective-permute-start | bytes 4718600 | tf_op jit(solution)/shard_map/ppermute | solution.py:31
  116.3 172.6 %collective-permute-start.9 = (bf16[512,1536]{1,0:T(8,128)(2,1)S(1)}, bf16[512,1536]{1,0:T(8,128)(2,1)}, u32[]{:S(2)}, u32[]{:S(2)}) collective-permute-start(bf16[512,1536]{1,0:T(8,128)(2,1)S(1)} %bitcast.202), channel_id=1, source_target_pairs={{0,3},{1,0},{2,1},{3,2},{4,7},{5,4},{6,5},{7,6},{8,11},{9,8},{10,9... | collective-permute-start | bytes 4718600 | tf_op jit(solution)/shard_map/ppermute | solution.py:32
  152.0 166.7 %collective-permute-start.12 = (bf16[512,1536]{1,0:T(8,128)(2,1)S(1)}, bf16[512,1536]{1,0:T(8,128)(2,1)}, u32[]{:S(2)}, u32[]{:S(2)}) collective-permute-start(bf16[512,1536]{1,0:T(8,128)(2,1)S(1)} %bitcast.191), channel_id=1, source_target_pairs={{0,1},{1,2},{2,3},{3,0},{4,5},{5,6},{6,7},{7,4},{8,9},{9,10},{10,1... | collective-permute-start | bytes 4718600 | tf_op jit(solution)/shard_map/ppermute | solution.py:31
  183.8 172.5 %collective-permute-start.13 = (bf16[512,1536]{1,0:T(8,128)(2,1)S(1)}, bf16[512,1536]{1,0:T(8,128)(2,1)}, u32[]{:S(2)}, u32[]{:S(2)}) collective-permute-start(bf16[512,1536]{1,0:T(8,128)(2,1)S(1)} %bitcast.192), channel_id=1, source_target_pairs={{0,3},{1,0},{2,1},{3,2},{4,7},{5,4},{6,5},{7,6},{8,11},{9,8},{10,9... | collective-permute-start | bytes 4718600 | tf_op jit(solution)/shard_map/ppermute | solution.py:32
  219.4 1.6 copy-start.3
  219.4 1.8 copy-start.4
  221.6 4.1 copy-start.5
  235.6 133.6 %collective-permute-start.2 = (bf16[256,1536]{1,0:T(8,128)(2,1)}, bf16[256,1536]{1,0:T(8,128)(2,1)}, u32[]{:S(2)}, u32[]{:S(2)}) collective-permute-start(bf16[256,1536]{1,0:T(8,128)(2,1)} %slice.134), channel_id=1, source_target_pairs={{0,1},{1,2},{2,3},{3,0},{4,5},{5,6},{6,7},{7,4},{8,9},{9,10},{10,1... | collective-permute-start | bytes 2359304 | tf_op jit(solution)/shard_map/ppermute | solution.py:28
  251.2 139.3 %collective-permute-start.3 = (bf16[256,1536]{1,0:T(8,128)(2,1)}, bf16[256,1536]{1,0:T(8,128)(2,1)}, u32[]{:S(2)}, u32[]{:S(2)}) collective-permute-start(bf16[256,1536]{1,0:T(8,128)(2,1)} %slice.135), channel_id=1, source_target_pairs={{0,3},{1,0},{2,1},{3,2},{4,7},{5,4},{6,5},{7,6},{8,11},{9,8},{10,9... | collective-permute-start | bytes 2359304 | tf_op jit(solution)/shard_map/ppermute | solution.py:29
  288.9 115.6 %collective-permute-start.6 = (bf16[256,1536]{1,0:T(8,128)(2,1)}, bf16[256,1536]{1,0:T(8,128)(2,1)}, u32[]{:S(2)}, u32[]{:S(2)}) collective-permute-start(bf16[256,1536]{1,0:T(8,128)(2,1)} %slice.142), channel_id=1, source_target_pairs={{0,1},{1,2},{2,3},{3,0},{4,5},{5,6},{6,7},{7,4},{8,9},{9,10},{10,1... | collective-permute-start | bytes 2359304 | tf_op jit(solution)/shard_map/ppermute | solution.py:28
  318.7 105.5 %collective-permute-start.7 = (bf16[256,1536]{1,0:T(8,128)(2,1)}, bf16[256,1536]{1,0:T(8,128)(2,1)}, u32[]{:S(2)}, u32[]{:S(2)}) collective-permute-start(bf16[256,1536]{1,0:T(8,128)(2,1)} %slice.143), channel_id=1, source_target_pairs={{0,3},{1,0},{2,1},{3,2},{4,7},{5,4},{6,5},{7,6},{8,11},{9,8},{10,9... | collective-permute-start | bytes 2359304 | tf_op jit(solution)/shard_map/ppermute | solution.py:29
  356.3 80.5 %collective-permute-start.10 = (bf16[256,1536]{1,0:T(8,128)(2,1)}, bf16[256,1536]{1,0:T(8,128)(2,1)}, u32[]{:S(2)}, u32[]{:S(2)}) collective-permute-start(bf16[256,1536]{1,0:T(8,128)(2,1)} %slice.150), channel_id=1, source_target_pairs={{0,1},{1,2},{2,3},{3,0},{4,5},{5,6},{6,7},{7,4},{8,9},{9,10},{10,1... | collective-permute-start | bytes 2359304 | tf_op jit(solution)/shard_map/ppermute | solution.py:28
  369.3 83.9 %collective-permute-start.11 = (bf16[256,1536]{1,0:T(8,128)(2,1)}, bf16[256,1536]{1,0:T(8,128)(2,1)}, u32[]{:S(2)}, u32[]{:S(2)}) collective-permute-start(bf16[256,1536]{1,0:T(8,128)(2,1)} %slice.151), channel_id=1, source_target_pairs={{0,3},{1,0},{2,1},{3,2},{4,7},{5,4},{6,5},{7,6},{8,11},{9,8},{10,9... | collective-permute-start | bytes 2359304 | tf_op jit(solution)/shard_map/ppermute | solution.py:29
  390.5 80.0 %collective-permute-start.14 = (bf16[256,1536]{1,0:T(8,128)(2,1)}, bf16[256,1536]{1,0:T(8,128)(2,1)}, u32[]{:S(2)}, u32[]{:S(2)}) collective-permute-start(bf16[256,1536]{1,0:T(8,128)(2,1)} %slice.158), channel_id=1, source_target_pairs={{0,1},{1,2},{2,3},{3,0},{4,5},{5,6},{6,7},{7,4},{8,9},{9,10},{10,1... | collective-permute-start | bytes 2359304 | tf_op jit(solution)/shard_map/ppermute | solution.py:28
  400.7 3.8 copy-start.6
  404.5 81.5 %collective-permute-start.15 = (bf16[256,1536]{1,0:T(8,128)(2,1)S(1)}, bf16[256,1536]{1,0:T(8,128)(2,1)S(1)}, u32[]{:S(2)}, u32[]{:S(2)}) collective-permute-start(bf16[256,1536]{1,0:T(8,128)(2,1)S(1)} %copy-done.6), channel_id=1, source_target_pairs={{0,3},{1,0},{2,1},{3,2},{4,7},{5,4},{6,5},{7,6},{8,11},{9,8},{10,9... | collective-permute-start | bytes 2359304 | tf_op jit(solution)/shard_map/ppermute | solution.py:29
  472.7 13.3 %copy-start = (f32[4,2,512,2048]{3,2,1,0:T(8,128)}, f32[4,2,512,2048]{3,2,1,0:T(8,128)S(1)}, u32[]{:S(2)}) copy-start(f32[4,2,512,2048]{3,2,1,0:T(8,128)S(1)} %fusion.19) | copy-start | bytes 100663296
where the time goes:
time: 489 us; the launch traced here: 488 us
  starting transfers between devices  203 us (42%)
  waiting for transfers between devices  167 us (34%)
  matrix products  57.7 us (12%)
  local copies, waits for them, and re-layouts  39 us (8%)
  other arithmetic  21.1 us (4%)
    ppermute x4, starting transfers between devices, ring_blocks(): lax.ppermute(from_right[half:], 'feed', backward)  107 us
    ppermute x4, starting transfers between devices, ring_blocks(): from_right = lax.ppermute(from_right, 'feed', backward)  77.5 us
    ppermute x4, waiting for transfers between devices, ring_blocks(): from_left = lax.ppermute(from_left, 'feed', forward)  77.4 us
    dot_general x20, matrix products, correlate(): jnp.einsum('qrk,fk->qrf', stacked, columns, preferred_element_type=jnp.fl...  57.7 us
    all_to_all x4, waiting for transfers between devices, per_device(): lax.all_to_all(blocks, 'freq', split_axis=0, concat_axis=0, tiled=True)  49.6 us
    ppermute x4, waiting for transfers between devices, ring_blocks(): lax.ppermute(from_right[half:], 'feed', backward)  27.6 us
    slice x1, local copies, waits for them, and re-layouts, per_device(): volt_imag = volts[:, channel, :, 1].astype(jnp.float32)  17.9 us
    all_to_all x4, starting transfers between devices, per_device(): lax.all_to_all(blocks, 'freq', split_axis=0, concat_axis=0, tiled=True)  16.6 us
  transfers between devices with their start and end apart: 20, of which 12 were waited for; matrix products, arithmetic and copies ran while one was open for 19% of the time, Pallas kernels for 0%

commit v1 on v0

--- a/solution.py
+++ b/solution.py
@@ -1,7 +1,16 @@
+import functools
+
 import jax
 import jax.numpy as jnp
 from jax import lax
+from jax.experimental import pallas as pl
+from jax.experimental.pallas import tpu as pltpu
 from jax.sharding import PartitionSpec as P
+
+MESH = pl.DeviceIdType.MESH
+ANY = pl.BlockSpec(memory_space=pl.ANY)
+VMEM = pl.BlockSpec(memory_space=pltpu.VMEM)
+
 
 def stack_rows(own_rows, samples):
     real_part = own_rows[..., :samples]
@@ -35,7 +44,7 @@
     return pieces
 
 
-def per_device(voltages, gains):
+def ring_program(voltages, gains):
     channels, local_feeds, _, samples = voltages.shape
     freq_count = lax.axis_size("freq")
     feed_count = lax.axis_size("feed")
@@ -66,9 +75,450 @@
     return visibilities
 
 
+def bit_flip(index, mask, count):
+    total, bit = 0, 1
+    while bit < count:
+        total = total + ((index // bit + mask // bit) % 2) * bit
+        bit *= 2
+    return total
+
+
+def line_kernel(
+    geometry,
+    volts,
+    scale,
+    out,
+    held,
+    staged,
+    landed,
+    wide,
+    raw,
+    sent,
+    raw_sem,
+    turn_send,
+    turn_recv,
+    out_send,
+    out_recv,
+    mid_send,
+    mid_recv,
+    vis_send,
+    vis_recv,
+    wide_sem,
+):
+    owned, freq_count, local_feeds, samples = geometry
+    rows = freq_count * local_feeds
+    pairs = freq_count // 2
+    chunk = 2 * local_feeds
+    stage_slots = staged.shape[0]
+    raw_slots = raw.shape[0]
+    blocks = owned * freq_count
+
+    me = lax.axis_index("freq")
+    plane = lax.axis_index("feed")
+    my_pair = me // 2
+    inner = (plane == 1) | (plane == 2)
+    across = 3 - plane
+    beside = jnp.where(plane < 2, 1 - plane, 5 - plane)
+
+    barrier = pltpu.get_barrier_semaphore()
+    for shift in range(1, freq_count):
+        pl.semaphore_signal(
+            barrier,
+            inc=1,
+            device_id=(bit_flip(me, shift, freq_count), plane),
+            device_id_type=MESH,
+        )
+    pl.semaphore_signal(barrier, inc=1, device_id=(me, beside), device_id_type=MESH)
+
+    @pl.when(inner)
+    def _():
+        pl.semaphore_signal(barrier, inc=1, device_id=(me, across), device_id_type=MESH)
+
+    def load(index):
+        channel, shift = index // freq_count, index % freq_count
+        owner = bit_flip(me, shift, freq_count)
+        return pltpu.make_async_copy(
+            volts.at[owner * owned + channel],
+            raw.at[index % raw_slots],
+            raw_sem.at[index % raw_slots],
+        )
+
+    for index in range(raw_slots):
+        load(index).start()
+
+    @pl.when(inner)
+    def _():
+        pl.semaphore_wait(barrier, freq_count + 1)
+
+    @pl.when(jnp.logical_not(inner))
+    def _():
+        pl.semaphore_wait(barrier, freq_count)
+
+    def turn(channel, owner):
+        return pltpu.make_async_remote_copy(
+            src_ref=sent.at[channel, owner],
+            dst_ref=held.at[0, channel, pl.ds(me * local_feeds, local_feeds)],
+            send_sem=turn_send.at[channel, owner],
+            recv_sem=turn_recv.at[channel, me],
+            device_id=(owner, plane),
+            device_id_type=MESH,
+        )
+
+    def turned(channel, source):
+        return pltpu.make_async_remote_copy(
+            src_ref=sent.at[channel, source],
+            dst_ref=held.at[0, channel, pl.ds(source * local_feeds, local_feeds)],
+            send_sem=turn_send.at[channel, source],
+            recv_sem=turn_recv.at[channel, source],
+            device_id=(source, plane),
+            device_id_type=MESH,
+        )
+
+    def equalize(index, put):
+        channel, shift = index // freq_count, index % freq_count
+        owner = bit_flip(me, shift, freq_count)
+        slot = index % raw_slots
+        load(index).wait()
+        which = owner * owned + channel
+        tile = 16
+        for start in range(0, local_feeds, tile):
+            gain_real = scale[0, which, pl.ds(start, tile), :]
+            gain_imag = scale[1, which, pl.ds(start, tile), :]
+            for lane in range(0, samples, 128):
+                real = raw[slot, pl.ds(start, tile), 0, pl.ds(lane, 128)].astype(jnp.float32)
+                imag = raw[slot, pl.ds(start, tile), 1, pl.ds(lane, 128)].astype(jnp.float32)
+                put(
+                    channel,
+                    owner,
+                    start,
+                    tile,
+                    lane,
+                    (gain_real * real - gain_imag * imag).astype(jnp.bfloat16),
+                    (gain_real * imag + gain_imag * real).astype(jnp.bfloat16),
+                )
+
+        @pl.when(index + raw_slots < blocks)
+        def _():
+            load(index + raw_slots).start()
+
+    def put_own(channel, owner, start, tile, lane, real, imag):
+        where = pl.ds(me * local_feeds + start, tile)
+        held[0, channel, where, pl.ds(lane, 128)] = real
+        held[0, channel, where, pl.ds(samples + lane, 128)] = imag
+
+    def put_sent(channel, owner, start, tile, lane, real, imag):
+        sent[channel, owner, pl.ds(start, tile), pl.ds(lane, 128)] = real
+        sent[channel, owner, pl.ds(start, tile), pl.ds(samples + lane, 128)] = imag
+
+    def equalize_channel(channel):
+        equalize(channel * freq_count, put_own)
+
+        @pl.loop(1, freq_count)
+        def _(shift):
+            equalize(channel * freq_count + shift, put_sent)
+            turn(channel, bit_flip(me, shift, freq_count)).start()
+
+    def rows_of(step):
+        return pl.ds(pl.multiple_of(bit_flip(my_pair, step, pairs) * chunk, chunk), chunk)
+
+    def sample_copy(channel, step, source, target, send, recv, device):
+        where = rows_of(step)
+        return pltpu.make_async_remote_copy(
+            src_ref=held.at[source, channel, where],
+            dst_ref=held.at[target, channel, where],
+            send_sem=send,
+            recv_sem=recv,
+            device_id=(me, device),
+            device_id_type=MESH,
+        )
+
+    def outward(channel, step):
+        return sample_copy(
+            channel, step, 0, 1, out_send.at[channel, step], out_recv.at[channel, step], beside
+        )
+
+    def middle(which, channel, step):
+        return sample_copy(
+            channel,
+            step,
+            which,
+            2 + which,
+            mid_send.at[which, channel, step],
+            mid_recv.at[which, channel, step],
+            across,
+        )
+
+    def await_turn(channel, step):
+        pair = bit_flip(my_pair, step, pairs)
+        for core in range(2):
+            source = pair * 2 + core
+
+            @pl.when(source != me)
+            def _():
+                turned(channel, source).wait_recv()
+
+    def pass_on(channel, step):
+        await_turn(channel, step)
+
+        @pl.when(inner)
+        def _():
+            middle(0, channel, step).start()
+
+        @pl.when(jnp.logical_not(inner))
+        def _():
+            outward(channel, step).start()
+
+    def product(left, right):
+        contract = (((1,), (1,)), ((), ()))
+        dot = functools.partial(
+            lax.dot_general, dimension_numbers=contract, preferred_element_type=jnp.float32
+        )
+        real = dot(left, right)
+        imag = dot(left[:, samples:], right[:, :samples]) - dot(left[:, :samples], right[:, samples:])
+        return real * (1.0 / samples), imag * (1.0 / samples)
+
+    equalize_channel(0)
+    pass_on(0, 0)
+
+    @pl.loop(1, owned)
+    def _(channel):
+        equalize_channel(channel)
+
+    @pl.loop(1, pairs)
+    def _(step):
+        pass_on(0, step)
+
+    def wide_copy(slot, channel, block):
+        return pltpu.make_async_copy(
+            wide.at[slot],
+            out.at[channel, :, :, pl.ds(pl.multiple_of(block * rows, rows), rows)],
+            wide_sem.at[slot],
+        )
+
+    def own_block(channel, source, block, count):
+        slot = count % 2
+
+        @pl.when(count >= 2)
+        def _():
+            wide_copy(slot, channel, block).wait()
+
+        size = min(256, rows)
+
+        @pl.loop(0, rows // size)
+        def _(i):
+            @pl.loop(0, rows // size)
+            def _(j):
+                real, imag = product(
+                    held[0, channel, pl.ds(i * size, size), :],
+                    held[source, channel, pl.ds(j * size, size), :],
+                )
+                wide[slot, 0, pl.ds(i * size, size), pl.ds(pl.multiple_of(j * size, size), size)] = real
+                wide[slot, 1, pl.ds(i * size, size), pl.ds(pl.multiple_of(j * size, size), size)] = imag
+
+        wide_copy(slot, channel, block).start()
+
+    def vis_copy(item, slot, channel, kind, step, across_columns):
+        where = rows_of(step)
+        if across_columns:
+            source = staged.at[slot, :, :, where]
+            target = landed.at[channel, kind, :, :, where]
+        else:
+            source = staged.at[slot, :, where, :]
+            target = landed.at[channel, kind, :, where, :]
+        return pltpu.make_async_remote_copy(
+            src_ref=source,
+            dst_ref=target,
+            send_sem=vis_send.at[slot, step],
+            recv_sem=vis_recv.at[channel, kind, step],
+            device_id=(me, beside),
+            device_id_type=MESH,
+        )
+
+    def claim(item):
+        @pl.when(item >= stage_slots)
+        def _():
+            for step in range(pairs):
+                vis_copy(item, item % stage_slots, 0, 0, step, False).wait_send()
+
+    def vis_rows(channel, kind, source, step):
+        item = channel * 3 + kind
+        slot = item % stage_slots
+        where = rows_of(step)
+        size = min(256, rows)
+
+        @pl.loop(0, rows // size)
+        def _(j):
+            columns = pl.ds(pl.multiple_of(j * size, size), size)
+            real, imag = product(held[1, channel, where, :], held[source, channel, columns, :])
+            staged[slot, 0, where, columns] = real.astype(jnp.bfloat16)
+            staged[slot, 1, where, columns] = imag.astype(jnp.bfloat16)
+
+        vis_copy(item, slot, channel, kind, step, False).start()
+
+    def vis_columns(channel, kind, source, step):
+        item = channel * 3 + kind
+        slot = item % stage_slots
+        where = rows_of(step)
+        size = min(256, rows)
+
+        @pl.loop(0, rows // size)
+        def _(i):
+            lines = pl.ds(pl.multiple_of(i * size, size), size)
+            real, imag = product(held[1, channel, lines, :], held[source, channel, where, :])
+            staged[slot, 0, lines, where] = real.astype(jnp.bfloat16)
+            staged[slot, 1, lines, where] = imag.astype(jnp.bfloat16)
+
+        vis_copy(item, slot, channel, kind, step, True).start()
+
+    @pl.when(inner)
+    def _():
+        @pl.loop(0, owned)
+        def _(channel):
+            claim(channel * 3)
+
+            @pl.loop(0, pairs)
+            def _(step):
+                outward(channel, step).wait_recv()
+                middle(1, channel, step).start()
+                vis_rows(channel, 0, 0, step)
+
+            @pl.when(channel + 1 < owned)
+            def _():
+                @pl.loop(0, pairs)
+                def _(step):
+                    await_turn(channel + 1, step)
+                    middle(0, channel + 1, step).start()
+
+            own_block(channel, 0, plane, channel * 4)
+            own_block(channel, 1, beside, channel * 4 + 1)
+
+            for step in range(pairs):
+                middle(0, channel, step).wait_recv()
+            claim(channel * 3 + 1)
+
+            @pl.loop(0, pairs)
+            def _(step):
+                vis_rows(channel, 1, 2, step)
+
+            own_block(channel, 2, across, channel * 4 + 2)
+            claim(channel * 3 + 2)
+
+            @pl.loop(0, pairs)
+            def _(step):
+                middle(1, channel, step).wait_recv()
+                vis_columns(channel, 2, 3, step)
+
+            own_block(channel, 3, 3 - beside, channel * 4 + 3)
+
+        for back in range(2):
+            wide_copy(back, 0, 0).wait()
+
+        @pl.loop(0, owned)
+        def _(channel):
+            for which in range(2):
+                for step in range(pairs):
+                    middle(which, channel, step).wait_send()
+
+        for slot in range(stage_slots):
+            for step in range(pairs):
+                vis_copy(0, slot, 0, 0, step, False).wait_send()
+
+    @pl.when(jnp.logical_not(inner))
+    def _():
+        @pl.loop(1, owned)
+        def _(channel):
+            @pl.loop(0, pairs)
+            def _(step):
+                await_turn(channel, step)
+                outward(channel, step).start()
+
+        @pl.loop(0, owned)
+        def _(channel):
+            own_block(channel, 0, plane, channel)
+
+        def widen(channel, kind, block, count):
+            slot = count % 2
+            wide_copy(slot, channel, block).wait()
+            across_columns = kind == 2
+
+            @pl.loop(0, pairs)
+            def _(step):
+                vis_copy(0, 0, channel, kind, step, across_columns).wait_recv()
+                where = rows_of(step)
+                for part in range(2):
+                    if across_columns:
+                        wide[slot, part, :, where] = landed[channel, kind, part, :, where].astype(jnp.float32)
+                    else:
+                        wide[slot, part, where, :] = landed[channel, kind, part, where, :].astype(jnp.float32)
+
+            wide_copy(slot, channel, block).start()
+
+        @pl.loop(0, owned)
+        def _(channel):
+            widen(channel, 0, beside, owned + channel * 3)
+            widen(channel, 1, 3 - beside, owned + channel * 3 + 1)
+            widen(channel, 2, across, owned + channel * 3 + 2)
+
+        for back in range(2):
+            wide_copy(back, 0, 0).wait()
+
+        @pl.loop(0, owned)
+        def _(channel):
+            for step in range(pairs):
+                outward(channel, step).wait_send()
+
+    @pl.loop(0, owned)
+    def _(channel):
+        @pl.loop(1, freq_count)
+        def _(shift):
+            turn(channel, bit_flip(me, shift, freq_count)).wait_send()
+
+
+def line_program(voltages, gains):
+    channels, local_feeds, _, samples = voltages.shape
+    freq_count = lax.axis_size("freq")
+    feed_count = lax.axis_size("feed")
+    owned = channels // freq_count
+    rows = local_feeds * freq_count
+    pairs = freq_count // 2
+    stage_slots = 3
+    raw_slots = 4
+    scale = jnp.broadcast_to(gains[..., None], gains.shape + (128,))
+    dma = pltpu.SemaphoreType.DMA
+    return pl.pallas_call(
+        functools.partial(line_kernel, (owned, freq_count, local_feeds, samples)),
+        name="line",
+        out_shape=jax.ShapeDtypeStruct((owned, 2, rows, rows * feed_count), jnp.float32),
+        in_specs=[ANY, VMEM],
+        out_specs=ANY,
+        scratch_shapes=[
+            pltpu.VMEM((4, owned, rows, 2 * samples), jnp.bfloat16),
+            pltpu.VMEM((stage_slots, 2, rows, rows), jnp.bfloat16),
+            pltpu.VMEM((owned, 3, 2, rows, rows), jnp.bfloat16),
+            pltpu.VMEM((2, 2, rows, rows), jnp.float32),
+            pltpu.VMEM((raw_slots, local_feeds, 2, samples), jnp.int32),
+            pltpu.VMEM((owned, freq_count, local_feeds, 2 * samples), jnp.bfloat16),
+            dma((raw_slots,)),
+            dma((owned, freq_count)),
+            dma((owned, freq_count)),
+            dma((owned, pairs)),
+            dma((owned, pairs)),
+            dma((2, owned, pairs)),
+            dma((2, owned, pairs)),
+            dma((stage_slots, pairs)),
+            dma((owned, 3, pairs)),
+            dma((2,)),
+        ],
+        compiler_params=pltpu.CompilerParams(
+            collective_id=0, has_side_effects=True, vmem_limit_bytes=67043328
+        ),
+    )(voltages, scale)
+
+
 def solution(mesh):
     in_specs = (P(None, ("feed", "freq"), None, None), P(None, None, ("feed", "freq")))
     out_specs = P("freq", None, "feed", None)
-    return jax.shard_map(
-        per_device, mesh=mesh, in_specs=in_specs, out_specs=out_specs, check_vma=False
-    )
+    freq_count = mesh.shape["freq"]
+    on_a_line = mesh.shape["feed"] == 4 and freq_count > 1 and freq_count & (freq_count - 1) == 0
+    body = line_program if on_a_line else ring_program
+    return jax.shard_map(body, mesh=mesh, in_specs=in_specs, out_specs=out_specs, check_vma=False)

time: 489 us -> 336 us (0.69)
  Pallas kernels: 0 us -> 309 us
  starting transfers between devices: 203 us -> 0 us
  waiting for transfers between devices: 167 us -> 0 us
  matrix products: 57.7 us -> 0 us
  other arithmetic: 21.1 us -> 0 us
  local copies, waits for them, and re-layouts: 39 us -> 25.8 us
    pallas_call x0 -> x1, Pallas kernels: none -> 309 us  [line_program(): pl.pallas_call(functools.partial(line_kernel, (owned, freq_count, local_f...]
    ppermute x16 -> x0, starting transfers between devices: 187 us -> none  [the longest x4 107 us: ring_blocks(): lax.ppermute(from_right[half:], 'feed', backward)]
    ppermute x16 -> x0, waiting for transfers between devices: 117 us -> none  [the longest x4 77.4 us: ring_blocks(): from_left = lax.ppermute(from_left, 'feed', forward)]
    dot_general x20 -> x0, matrix products: 57.7 us -> none  [correlate(): jnp.einsum('qrk,fk->qrf', stacked, columns, preferred_element_type=jnp.fl...]
    all_to_all x4 -> x0, waiting for transfers between devices: 49.6 us -> none  [per_device(): lax.all_to_all(blocks, 'freq', split_axis=0, concat_axis=0, tiled=True)]
    slice x10 -> x0, local copies, waits for them, and re-layouts: 34.6 us -> none  [the longest x1 17.9 us: per_device(): volt_imag = volts[:, channel, :, 1].astype(jnp.float32)]
    unnamed x16 -> x1, local copies, waits for them, and re-layouts: 0.26 us -> 23.2 us
    all_to_all x4 -> x0, starting transfers between devices: 16.6 us -> none  [per_device(): lax.all_to_all(blocks, 'freq', split_axis=0, concat_axis=0, tiled=True)]
  transfers between devices with their start and end apart: 20 -> 0, of which waited for: 12 -> 0; matrix products, arithmetic and copies ran while one was open for 19% -> 0% of each run, Pallas kernels for 0% -> 0%
where the time goes in v1:
time: 336 us; the launch traced here: 335 us
  Pallas kernels  309 us (92%)
  local copies, waits for them, and re-layouts  25.8 us (8%)
    pallas_call x1, Pallas kernels, line_program(): pl.pallas_call(functools.partial(line_kernel, (owned, freq_count, local_f...  309 us
    unnamed x1, local copies, waits for them, and re-layouts  23.2 us

profile of v1, /device:TPU:0, one launch (start us, length us, event | category | flops | bytes accessed | tf_op | source)
XLA Modules:
  0.0 335.3 jit_solution(435902634548756457)
XLA Ops:
  0.0 2.7 broadcast_in_dim.2.scale
  2.7 309.4 %line.1 = f32[4,2,512,2048]{3,2,1,0:T(8,128)} custom-call(s32[32,64,2,768]{3,2,1,0:T(2,128)} %volts.1, f32[2,32,64,128]{3,2,1,0:T(8,128)} %broadcast_in_dim.2.scale), custom_call_target="tpu_custom_call" | custom-call | tf_op jit(solution)/shard_map/line/pallas_call | solution.py:488
  312.1 23.2 %copy.4 = f32[4,2,512,2048]{3,2,1,0:T(8,128)} copy(f32[4,2,512,2048]{3,2,1,0:T(8,128)} %line.1) | data formatting | bytes 67108864

commit v2 on v1

--- a/solution.py
+++ b/solution.py
@@ -86,14 +86,15 @@
 def line_kernel(
     geometry,
     volts,
-    scale,
-    out,
+    gains,
+    landed,
+    full,
     held,
     staged,
-    landed,
     wide,
     raw,
     sent,
+    scale,
     raw_sem,
     turn_send,
     turn_recv,
@@ -101,6 +102,8 @@
     out_recv,
     mid_send,
     mid_recv,
+    in_send,
+    in_recv,
     vis_send,
     vis_recv,
     wide_sem,
@@ -109,9 +112,10 @@
     rows = freq_count * local_feeds
     pairs = freq_count // 2
     chunk = 2 * local_feeds
-    stage_slots = staged.shape[0]
     raw_slots = raw.shape[0]
     blocks = owned * freq_count
+    channels = blocks
+    early = min(2, owned - 1)
 
     me = lax.axis_index("freq")
     plane = lax.axis_index("feed")
@@ -145,6 +149,10 @@
 
     for index in range(raw_slots):
         load(index).start()
+
+    columns = jnp.transpose(gains[...])
+    for which in range(scale.shape[0]):
+        scale[which] = jnp.broadcast_to(columns[:local_feeds, which : which + 1], (local_feeds, 128))
 
     @pl.when(inner)
     def _():
@@ -182,8 +190,8 @@
         which = owner * owned + channel
         tile = 16
         for start in range(0, local_feeds, tile):
-            gain_real = scale[0, which, pl.ds(start, tile), :]
-            gain_imag = scale[1, which, pl.ds(start, tile), :]
+            gain_real = scale[which, pl.ds(start, tile), :]
+            gain_imag = scale[channels + which, pl.ds(start, tile), :]
             for lane in range(0, samples, 128):
                 real = raw[slot, pl.ds(start, tile), 0, pl.ds(lane, 128)].astype(jnp.float32)
                 imag = raw[slot, pl.ds(start, tile), 1, pl.ds(lane, 128)].astype(jnp.float32)
@@ -210,13 +218,15 @@
         sent[channel, owner, pl.ds(start, tile), pl.ds(lane, 128)] = real
         sent[channel, owner, pl.ds(start, tile), pl.ds(samples + lane, 128)] = imag
 
-    def equalize_channel(channel):
-        equalize(channel * freq_count, put_own)
-
-        @pl.loop(1, freq_count)
+    def equalize_some(channel, first, last):
+        @pl.loop(first, last)
         def _(shift):
             equalize(channel * freq_count + shift, put_sent)
             turn(channel, bit_flip(me, shift, freq_count)).start()
+
+    def equalize_channel(channel):
+        equalize(channel * freq_count, put_own)
+        equalize_some(channel, 1, freq_count)
 
     def rows_of(step):
         return pl.ds(pl.multiple_of(bit_flip(my_pair, step, pairs) * chunk, chunk), chunk)
@@ -248,6 +258,12 @@
             across,
         )
 
+    def inward(channel):
+        return sample_copy(channel, 0, 0, 2, in_send.at[channel], in_recv.at[channel], beside)
+
+    def is_early(channel):
+        return (channel >= 1) & (channel <= early)
+
     def await_turn(channel, step):
         pair = bit_flip(my_pair, step, pairs)
         for core in range(2):
@@ -277,72 +293,95 @@
         imag = dot(left[:, samples:], right[:, :samples]) - dot(left[:, :samples], right[:, samples:])
         return real * (1.0 / samples), imag * (1.0 / samples)
 
-    equalize_channel(0)
+    first = max(freq_count // 2, 2)
+    equalize(0, put_own)
+    equalize_some(0, 1, first)
     pass_on(0, 0)
-
-    @pl.loop(1, owned)
-    def _(channel):
+    equalize_some(0, first, freq_count)
+
+    def equalize_early(channel):
         equalize_channel(channel)
-
-    @pl.loop(1, pairs)
+        await_turn(channel, 0)
+
+        @pl.when(inner)
+        def _():
+            inward(channel).start()
+
+    pl.loop(1, early + 1)(equalize_early)
+
+    @pl.loop(1, pairs // 2 + 1)
     def _(step):
         pass_on(0, step)
 
-    def wide_copy(slot, channel, block):
-        return pltpu.make_async_copy(
-            wide.at[slot],
-            out.at[channel, :, :, pl.ds(pl.multiple_of(block * rows, rows), rows)],
-            wide_sem.at[slot],
-        )
-
-    def own_block(channel, source, block, count):
-        slot = count % 2
-
-        @pl.when(count >= 2)
-        def _():
-            wide_copy(slot, channel, block).wait()
-
+    pl.loop(early + 1, owned)(equalize_channel)
+
+    @pl.loop(pairs // 2 + 1, pairs)
+    def _(step):
+        pass_on(0, step)
+
+    def wide_copy(slot, channel, kind):
+        return pltpu.make_async_copy(wide.at[slot], full.at[channel, kind], wide_sem.at[slot])
+
+    def own_block(channel, source, put):
         size = min(256, rows)
 
         @pl.loop(0, rows // size)
         def _(i):
             @pl.loop(0, rows // size)
             def _(j):
-                real, imag = product(
-                    held[0, channel, pl.ds(i * size, size), :],
-                    held[source, channel, pl.ds(j * size, size), :],
-                )
-                wide[slot, 0, pl.ds(i * size, size), pl.ds(pl.multiple_of(j * size, size), size)] = real
-                wide[slot, 1, pl.ds(i * size, size), pl.ds(pl.multiple_of(j * size, size), size)] = imag
-
-        wide_copy(slot, channel, block).start()
-
-    def vis_copy(item, slot, channel, kind, step, across_columns):
+                lines = pl.ds(pl.multiple_of(i * size, size), size)
+                where = pl.ds(pl.multiple_of(j * size, size), size)
+                real, imag = product(held[0, channel, lines, :], held[source, channel, where, :])
+                put(0, lines, where, real)
+                put(1, lines, where, imag)
+
+    def own_full(channel, source, kind):
+        @pl.when(channel >= 1)
+        def _():
+            wide_copy(kind, channel, kind).wait()
+
+        def put(part, lines, where, value):
+            wide[kind, part, lines, where] = value
+
+        own_block(channel, source, put)
+        wide_copy(kind, channel, kind).start()
+
+    def own_half(channel, source, kind):
+        def put(part, lines, where, value):
+            landed[channel, kind, part, lines, where] = value.astype(jnp.bfloat16)
+
+        own_block(channel, source, put)
+
+    def vis_copy(channel, kind, step, across_columns):
         where = rows_of(step)
         if across_columns:
-            source = staged.at[slot, :, :, where]
+            source = staged.at[kind, :, :, where]
             target = landed.at[channel, kind, :, :, where]
         else:
-            source = staged.at[slot, :, where, :]
+            source = staged.at[kind, :, where, :]
             target = landed.at[channel, kind, :, where, :]
         return pltpu.make_async_remote_copy(
             src_ref=source,
             dst_ref=target,
-            send_sem=vis_send.at[slot, step],
+            send_sem=vis_send.at[kind, step],
             recv_sem=vis_recv.at[channel, kind, step],
             device_id=(me, beside),
             device_id_type=MESH,
         )
 
-    def claim(item):
-        @pl.when(item >= stage_slots)
+    def release(channel, kind):
+        for step in range(pairs):
+
+            @pl.when(jnp.logical_not((step == 0) & (kind == 0) & is_early(channel)))
+            def _():
+                vis_copy(channel, kind, step, False).wait_send()
+
+    def claim(channel, kind):
+        @pl.when(channel >= 1)
         def _():
-            for step in range(pairs):
-                vis_copy(item, item % stage_slots, 0, 0, step, False).wait_send()
+            release(channel - 1, kind)
 
     def vis_rows(channel, kind, source, step):
-        item = channel * 3 + kind
-        slot = item % stage_slots
         where = rows_of(step)
         size = min(256, rows)
 
@@ -350,14 +389,12 @@
         def _(j):
             columns = pl.ds(pl.multiple_of(j * size, size), size)
             real, imag = product(held[1, channel, where, :], held[source, channel, columns, :])
-            staged[slot, 0, where, columns] = real.astype(jnp.bfloat16)
-            staged[slot, 1, where, columns] = imag.astype(jnp.bfloat16)
-
-        vis_copy(item, slot, channel, kind, step, False).start()
+            staged[kind, 0, where, columns] = real.astype(jnp.bfloat16)
+            staged[kind, 1, where, columns] = imag.astype(jnp.bfloat16)
+
+        vis_copy(channel, kind, step, False).start()
 
     def vis_columns(channel, kind, source, step):
-        item = channel * 3 + kind
-        slot = item % stage_slots
         where = rows_of(step)
         size = min(256, rows)
 
@@ -365,53 +402,64 @@
         def _(i):
             lines = pl.ds(pl.multiple_of(i * size, size), size)
             real, imag = product(held[1, channel, lines, :], held[source, channel, where, :])
-            staged[slot, 0, lines, where] = real.astype(jnp.bfloat16)
-            staged[slot, 1, lines, where] = imag.astype(jnp.bfloat16)
-
-        vis_copy(item, slot, channel, kind, step, True).start()
+            staged[kind, 0, lines, where] = real.astype(jnp.bfloat16)
+            staged[kind, 1, lines, where] = imag.astype(jnp.bfloat16)
+
+        vis_copy(channel, kind, step, True).start()
 
     @pl.when(inner)
     def _():
         @pl.loop(0, owned)
         def _(channel):
-            claim(channel * 3)
-
             @pl.loop(0, pairs)
             def _(step):
                 outward(channel, step).wait_recv()
                 middle(1, channel, step).start()
-                vis_rows(channel, 0, 0, step)
+
+                @pl.when(channel == 0)
+                def _():
+                    vis_rows(channel, 0, 0, step)
+
+            @pl.when(channel >= 1)
+            def _():
+                claim(channel, 0)
+
+                @pl.loop(jnp.where(is_early(channel), 1, 0), pairs)
+                def _(step):
+                    vis_columns(channel, 0, 0, step)
 
             @pl.when(channel + 1 < owned)
             def _():
                 @pl.loop(0, pairs)
                 def _(step):
-                    await_turn(channel + 1, step)
+                    @pl.when(jnp.logical_not((step == 0) & is_early(channel + 1)))
+                    def _():
+                        await_turn(channel + 1, step)
+
                     middle(0, channel + 1, step).start()
-
-            own_block(channel, 0, plane, channel * 4)
-            own_block(channel, 1, beside, channel * 4 + 1)
 
             for step in range(pairs):
                 middle(0, channel, step).wait_recv()
-            claim(channel * 3 + 1)
+            claim(channel, 1)
 
             @pl.loop(0, pairs)
             def _(step):
                 vis_rows(channel, 1, 2, step)
 
-            own_block(channel, 2, across, channel * 4 + 2)
-            claim(channel * 3 + 2)
+            own_full(channel, 0, 0)
+            own_full(channel, 1, 1)
+            own_half(channel, 2, 0)
+            claim(channel, 2)
 
             @pl.loop(0, pairs)
             def _(step):
                 middle(1, channel, step).wait_recv()
                 vis_columns(channel, 2, 3, step)
 
-            own_block(channel, 3, 3 - beside, channel * 4 + 3)
-
-        for back in range(2):
-            wide_copy(back, 0, 0).wait()
+            own_half(channel, 3, 1)
+
+        for kind in range(2):
+            wide_copy(kind, 0, kind).wait()
 
         @pl.loop(0, owned)
         def _(channel):
@@ -419,9 +467,12 @@
                 for step in range(pairs):
                     middle(which, channel, step).wait_send()
 
-        for slot in range(stage_slots):
-            for step in range(pairs):
-                vis_copy(0, slot, 0, 0, step, False).wait_send()
+        @pl.loop(1, early + 1)
+        def _(channel):
+            inward(channel).wait_send()
+
+        for kind in range(3):
+            release(owned - 1, kind)
 
     @pl.when(jnp.logical_not(inner))
     def _():
@@ -429,38 +480,42 @@
         def _(channel):
             @pl.loop(0, pairs)
             def _(step):
-                await_turn(channel, step)
+                @pl.when(jnp.logical_not((step == 0) & is_early(channel)))
+                def _():
+                    await_turn(channel, step)
+
                 outward(channel, step).start()
 
         @pl.loop(0, owned)
         def _(channel):
-            own_block(channel, 0, plane, channel)
-
-        def widen(channel, kind, block, count):
-            slot = count % 2
-            wide_copy(slot, channel, block).wait()
-            across_columns = kind == 2
-
-            @pl.loop(0, pairs)
-            def _(step):
-                vis_copy(0, 0, channel, kind, step, across_columns).wait_recv()
-                where = rows_of(step)
-                for part in range(2):
-                    if across_columns:
-                        wide[slot, part, :, where] = landed[channel, kind, part, :, where].astype(jnp.float32)
-                    else:
-                        wide[slot, part, where, :] = landed[channel, kind, part, where, :].astype(jnp.float32)
-
-            wide_copy(slot, channel, block).start()
-
-        @pl.loop(0, owned)
-        def _(channel):
-            widen(channel, 0, beside, owned + channel * 3)
-            widen(channel, 1, 3 - beside, owned + channel * 3 + 1)
-            widen(channel, 2, across, owned + channel * 3 + 2)
-
-        for back in range(2):
-            wide_copy(back, 0, 0).wait()
+            own_full(channel, 0, 0)
+
+        @pl.loop(0, owned)
+        def _(channel):
+            @pl.when(channel == 0)
+            def _():
+                for step in range(pairs):
+                    vis_copy(channel, 0, step, False).wait_recv()
+
+            @pl.when(channel >= 1)
+            def _():
+                @pl.when(is_early(channel))
+                def _():
+                    inward(channel).wait_recv()
+                    where = rows_of(0)
+                    real, imag = product(held[0, channel], held[2, channel, where, :])
+                    landed[channel, 0, 0, :, where] = real.astype(jnp.bfloat16)
+                    landed[channel, 0, 1, :, where] = imag.astype(jnp.bfloat16)
+
+                @pl.loop(jnp.where(is_early(channel), 1, 0), pairs)
+                def _(step):
+                    vis_copy(channel, 0, step, True).wait_recv()
+
+            for kind in range(1, 3):
+                for step in range(pairs):
+                    vis_copy(channel, kind, step, kind == 2).wait_recv()
+
+        wide_copy(0, 0, 0).wait()
 
         @pl.loop(0, owned)
         def _(channel):
@@ -481,23 +536,24 @@
     owned = channels // freq_count
     rows = local_feeds * freq_count
     pairs = freq_count // 2
-    stage_slots = 3
     raw_slots = 4
-    scale = jnp.broadcast_to(gains[..., None], gains.shape + (128,))
     dma = pltpu.SemaphoreType.DMA
-    return pl.pallas_call(
+    half, full = pl.pallas_call(
         functools.partial(line_kernel, (owned, freq_count, local_feeds, samples)),
         name="line",
-        out_shape=jax.ShapeDtypeStruct((owned, 2, rows, rows * feed_count), jnp.float32),
+        out_shape=[
+            pltpu.VMEM((owned, 3, 2, rows, rows), jnp.bfloat16),
+            jax.ShapeDtypeStruct((owned, 2, 2, rows, rows), jnp.float32),
+        ],
         in_specs=[ANY, VMEM],
-        out_specs=ANY,
+        out_specs=[VMEM, ANY],
         scratch_shapes=[
             pltpu.VMEM((4, owned, rows, 2 * samples), jnp.bfloat16),
-            pltpu.VMEM((stage_slots, 2, rows, rows), jnp.bfloat16),
-            pltpu.VMEM((owned, 3, 2, rows, rows), jnp.bfloat16),
+            pltpu.VMEM((3, 2, rows, rows), jnp.bfloat16),
             pltpu.VMEM((2, 2, rows, rows), jnp.float32),
             pltpu.VMEM((raw_slots, local_feeds, 2, samples), jnp.int32),
             pltpu.VMEM((owned, freq_count, local_feeds, 2 * samples), jnp.bfloat16),
+            pltpu.VMEM((2 * channels, local_feeds, 128), jnp.float32),
             dma((raw_slots,)),
             dma((owned, freq_count)),
             dma((owned, freq_count)),
@@ -505,14 +561,112 @@
             dma((owned, pairs)),
             dma((2, owned, pairs)),
             dma((2, owned, pairs)),
-            dma((stage_slots, pairs)),
+            dma((owned,)),
+            dma((owned,)),
+            dma((3, pairs)),
             dma((owned, 3, pairs)),
             dma((2,)),
         ],
         compiler_params=pltpu.CompilerParams(
-            collective_id=0, has_side_effects=True, vmem_limit_bytes=67043328
+            collective_id=0, has_side_effects=True, vmem_limit_bytes=48 * 2**20
         ),
-    )(voltages, scale)
+    )(voltages, gains.reshape(2 * channels, local_feeds))
+    return lay_out(half, full, feed_count)
+
+
+def lay_out_kernel(narrow, full, out, kept, wide, kept_sem, wide_sem, out_sem):
+    owned, _, _, rows, _ = narrow.shape
+    slots = wide.shape[0]
+    plane = lax.axis_index("feed")
+    inner = (plane == 1) | (plane == 2)
+    beside = jnp.where(plane < 2, 1 - plane, 5 - plane)
+    across, beyond = 3 - plane, 3 - beside
+
+    def kept_load(channel, kind):
+        return pltpu.make_async_copy(
+            full.at[channel, kind], kept.at[channel, kind], kept_sem.at[channel, kind]
+        )
+
+    def columns(channel, block):
+        return out.at[channel, :, :, pl.ds(pl.multiple_of(block * rows, rows), rows)]
+
+    def kept_store(channel, kind, block):
+        return pltpu.make_async_copy(
+            kept.at[channel, kind], columns(channel, block), out_sem.at[channel, kind]
+        )
+
+    def wide_store(slot, channel, block):
+        return pltpu.make_async_copy(wide.at[slot], columns(channel, block), wide_sem.at[slot])
+
+    def run(kept_blocks, narrow_blocks):
+        @pl.loop(0, owned)
+        def _(channel):
+            for kind in range(len(kept_blocks)):
+                kept_load(channel, kind).start()
+
+        count = len(narrow_blocks)
+
+        @pl.loop(0, owned)
+        def _(channel):
+            for kind, block in enumerate(kept_blocks):
+                kept_load(channel, kind).wait()
+                kept_store(channel, kind, block).start()
+            for kind, block in enumerate(narrow_blocks):
+                item = channel * count + kind
+                slot = item % slots
+
+                @pl.when(item >= slots)
+                def _():
+                    wide_store(slot, channel, block).wait()
+
+                tile = 64
+
+                @pl.loop(0, rows // tile)
+                def _(i):
+                    lines = pl.ds(pl.multiple_of(i * tile, tile), tile)
+                    for part in range(2):
+                        wide[slot, part, lines, :] = narrow[channel, kind, part, lines, :].astype(
+                            jnp.float32
+                        )
+
+                wide_store(slot, channel, block).start()
+
+        @pl.loop(0, owned)
+        def _(channel):
+            for kind, block in enumerate(kept_blocks):
+                kept_store(channel, kind, block).wait()
+
+        for slot in range(min(slots, owned * count)):
+            wide_store(slot, 0, narrow_blocks[0]).wait()
+
+    @pl.when(inner)
+    def _():
+        run([plane, beside], [across, beyond])
+
+    @pl.when(jnp.logical_not(inner))
+    def _():
+        run([plane], [beside, beyond, across])
+
+
+def lay_out(half, full, feed_count):
+    owned, _, _, rows, _ = half.shape
+    slots = 4
+    dma = pltpu.SemaphoreType.DMA
+    return pl.pallas_call(
+        lay_out_kernel,
+        name="lay_out",
+        out_shape=jax.ShapeDtypeStruct((owned, 2, rows, rows * feed_count), jnp.float32),
+        in_specs=[VMEM, ANY],
+        out_specs=ANY,
+        scratch_shapes=[
+            pltpu.VMEM(full.shape, full.dtype),
+            pltpu.VMEM((slots, 2, rows, rows), jnp.float32),
+            dma((owned, 2)),
+            dma((slots,)),
+            dma((owned, 2)),
+        ],
+        compiler_params=pltpu.CompilerParams(vmem_limit_bytes=40 * 2**20),
+    )(half, full)
 
 
 def solution(mesh):

time: 336 us -> 312 us (0.929)
  local copies, waits for them, and re-layouts: 25.8 us -> 0 us
    unnamed x1 -> x0, local copies, waits for them, and re-layouts: 23.2 us -> none
    pallas_call x0 -> x1, Pallas kernels: none -> 13.1 us  [lay_out(): pl.pallas_call(lay_out_kernel, name='lay_out', out_shape=jax.ShapeDtypeSt...]
    pallas_call x1, Pallas kernels: 309 us -> 298 us  [line_program(): pl.pallas_call(functools.partial(line_kernel, (owned, freq_count, local_f...]
where the time goes in v2:
time: 312 us; the launch traced here: 311 us
  Pallas kernels  311 us (100%)
    pallas_call x1, Pallas kernels, line_program(): pl.pallas_call(functools.partial(line_kernel, (owned, freq_count, local_f...  298 us
    pallas_call x1, Pallas kernels, lay_out(): pl.pallas_call(lay_out_kernel, name='lay_out', out_shape=jax.ShapeDtypeSt...  13.1 us

profile of v2, /device:TPU:0, one launch (start us, length us, event | category | flops | bytes accessed | tf_op | source)
XLA Modules:
  0.0 311.1 jit_solution(3166624401812380593)
XLA Ops:
  0.0 298.1 %line.1 = (bf16[4,3,2,512,512]{4,3,2,1,0:T(8,128)(2,1)S(1)}, f32[4,2,2,512,512]{4,3,2,1,0:T(8,128)}) custom-call(s32[32,64,2,768]{3,2,1,0:T(2,128)} %volts.1, f32[64,64]{1,0:T(8,128)} %bitcast.1), custom_call_target="tpu_custom_call" | custom-call | tf_op jit(solution)/shard_map/line/pallas_call | solution.py:541
  298.1 13.1 %lay_out.1 = f32[4,2,512,2048]{3,2,1,0:T(8,128)} custom-call(bf16[4,3,2,512,512]{4,3,2,1,0:T(8,128)(2,1)S(1)} %get-tuple-element.7.narrow, f32[4,2,2,512,512]{4,3,2,1,0:T(8,128)} %get-tuple-element.8.full), custom_call_target="tpu_custom_call" | custom-call | tf_op jit(solution)/shard_map/lay_out/pallas_call | solution.py:655
